TPU v7x, 32 devices: a whole 2x2x4 slice. The times are simulated.
32 devices in a mesh: member: 2 (over y), lat: 4 (over x, core), lon: 4 (over z).
Axes of the slice: x: 2, y: 2, z: 4, core: 2. Of those that a mesh axis runs over, the one named last changes fastest.
Arguments:
- field: bfloat16 [256, 512, 256], P(('member', 'lat'), 'lon'), parts along dimension 0, may hold values from -6 to 6
- mode_table: int32 [48], replicated, may hold values from 0 to 47, as said below
- analysis: bfloat16 [48, 48, 128], P(('lat', 'lon')), as said below
- synthesis: bfloat16 [48, 48, 128], P(('lat', 'lon')), as said below
- mixing: bfloat16 [1, 2, 256, 256], replicated, may hold values from -0.25 to 0.25
- degree_gain: float32 [1, 48, 256], replicated, may hold values from 0.25 to 1.75
- skip_weight: bfloat16 [1, 256, 256], replicated, may hold values from -0.375 to 0.375
Outputs:
- advanced: bfloat16 [256, 512, 256], P(('member', 'lat'), 'lon'), parts along dimension 0
- spectrum: bfloat16 [96, 48, 2, 256], P(('member', 'lat', 'lon')), parts along dimension 0
There are 2 independent parts, one for each index of `member`. A program takes and returns all parts, laid end to end along the dimension named above; an argument that names none is the same for every part. Nothing has to cross between parts.
Inputs may be any that keep to these rules, and one draw needn't show every extreme that they name: A permutation of 0 to 47; slot s of the spectral layout holds zonal wavenumber mode_table[s]. analysis[s, l, j] = weight[j] P(l, m, colat[j]) rounded to bfloat16, with m = mode_table[s], colat[j] = pi (j + 0.5) / 128, weight[j] = 2 pi^2 sin(colat[j]) / 65536, and P the orthonormal associated Legendre function of degree l and order m at cos(colat) without the Condon-Shortley phase, zero for l < m. synthesis[s, l, j] = c P(l, m, colat[j]) rounded to bfloat16, with m = mode_table[s], c = 1 where m = 0 and c = 2 elsewhere, P and colat as for analysis.
All inputs are finite; a program needn't handle non-finite values.
Results may differ from a plain program's by a relative error of at most 0.0062.
Values may be sent and summed in bfloat16 or wider, within the bound.
A program may use at most 64 MiB of HBM per device.

v0:
```python
import math
import jax
import jax.numpy as jnp
from jax import lax
from jax.sharding import PartitionSpec as P


def fourier_table(orders, length):
    phases = orders[:, None] * jnp.arange(length, dtype=jnp.int32)[None, :] % length
    angles = phases.astype(jnp.float32) * (2.0 * math.pi / length)
    return (
        jnp.stack([jnp.cos(angles), -jnp.sin(angles)], axis=1)
        .reshape(2 * orders.shape[0], length)
        .astype(jnp.bfloat16)
    )


def update(current, spectral, skip_matrix):
    shape_lead = current.shape
    direct = jnp.dot(
        current.reshape(-1, shape_lead[-1]), skip_matrix, preferred_element_type=jnp.float32
    ).reshape(shape_lead)
    pre_act = spectral.astype(jnp.float32) + direct
    return (current.astype(jnp.float32) + jax.nn.gelu(pre_act, approximate=False)).astype(
        jnp.bfloat16
    )


def per_device(field, mode_table, analysis, synthesis, mixing, degree_gain, skip_weight):
    lat_count = lax.axis_size("lat")
    lon_count = lax.axis_size("lon")
    lat_dev, lon_dev, channels = field.shape
    rows_full = lat_dev * lat_count
    points = lon_dev * lon_count
    mode_count = mode_table.shape[0]
    per_group = analysis.shape[0]
    forward = fourier_table(mode_table, points)
    mixed_last = None
    current = field
    row_block = lax.all_to_all(current, "lon", split_axis=0, concat_axis=1, tiled=True)
    lat_side = jnp.einsum(
        "rkc,qk->rqc", row_block, forward, preferred_element_type=jnp.float32
    ).astype(jnp.bfloat16)
    gathered = lax.all_to_all(lat_side, ("lat", "lon"), split_axis=1, concat_axis=0, tiled=True)
    lat_data = gathered.reshape(rows_full, per_group, 2 * channels)
    coefficients = jnp.einsum(
        "slj,jsx->slx", analysis, lat_data, preferred_element_type=jnp.float32
    ).astype(jnp.bfloat16)
    real_part = mixing[0, 0]
    imag_part = mixing[0, 1]
    joined = jnp.concatenate(
        [
            jnp.concatenate([real_part, imag_part], axis=1),
            jnp.concatenate([-imag_part, real_part], axis=1),
        ],
        axis=0,
    )
    product = jnp.dot(
        coefficients.reshape(-1, 2 * channels), joined, preferred_element_type=jnp.float32
    )
    product = product.reshape(per_group, mode_count, 2, channels)
    mixed_modes = (product * degree_gain[0][None, :, None, :]).astype(jnp.bfloat16)
    synthesized = jnp.einsum(
        "slj,slx->jsx",
        synthesis,
        mixed_modes.reshape(per_group, mode_count, 2 * channels),
        preferred_element_type=jnp.float32,
    )
    synthesized = synthesized.astype(jnp.bfloat16).reshape(rows_full, 2 * per_group, channels)
    returned = lax.all_to_all(synthesized, ("lat", "lon"), split_axis=0, concat_axis=1, tiled=True)
    spectral = jnp.einsum(
        "rqc,qk->rkc", returned, forward, preferred_element_type=jnp.float32
    ).astype(jnp.bfloat16)
    spectral, mixed_last = (spectral, mixed_modes)
    grid_part = lax.all_to_all(spectral, "lon", split_axis=1, concat_axis=0, tiled=True)
    current = update(current, grid_part, skip_weight[0])
    return (current, mixed_last)


def solution(mesh):
    in_specs = (
        P(("member", "lat"), "lon", None),
        P(),
        P(("lat", "lon"), None, None),
        P(("lat", "lon"), None, None),
        P(),
        P(),
        P(),
    )
    out_specs = (P(("member", "lat"), "lon", None), P(("member", "lat", "lon"), None, None, None))
    return jax.shard_map(
        per_device, mesh=mesh, in_specs=in_specs, out_specs=out_specs, check_vma=False
    )
```

profile of v0, /device:TPU:0, one launch (start us, length us, event | category | flops | bytes accessed | tf_op | source)
XLA Modules:
  0.0 162.0 jit_solution(3721329665403770944)
XLA Ops:
  0.7 6.5 %all-to-all-start = ((bf16[32,128,256]{2,1,0:T(8,128)(2,1)}), bf16[32,128,256]{2,1,0:T(8,128)(2,1)S(1)}, u32[]{:S(2)}, u32[]{:S(2)}) async-start(bf16[32,128,256]{2,1,0:T(8,128)(2,1)} %param.7), calls=%async_computation | async-start | bytes 4194304 | tf_op jit(solution)/shard_map/all_to_all | solution.py:40
  7.1 0.5 cosine_convert_fusion
  7.6 0.1 copy.50
  7.8 47.5 %all-to-all-done = bf16[32,128,256]{2,1,0:T(8,128)(2,1)S(1)} async-done(((bf16[32,128,256]{2,1,0:T(8,128)(2,1)}), bf16[32,128,256]{2,1,0:T(8,128)(2,1)S(1)}, u32[]{:S(2)}, u32[]{:S(2)}) %all-to-all-start) | async-done | bytes 2097184 | tf_op jit(solution)/shard_map/all_to_all | solution.py:40
  55.3 0.1 copy.51
  55.5 0.5 fusion.11
  56.0 1.0 copy.52
  57.0 3.8 %all-to-all-start.1 = ((bf16[8,96,256]{2,0,1:T(8,128)(2,1)}), bf16[8,96,256]{2,0,1:T(8,128)(2,1)S(1)}, u32[]{:S(2)}, u32[]{:S(2)}) async-start(bf16[8,96,256]{2,0,1:T(8,128)(2,1)} %copy.52), calls=%async_computation.1 | async-start | bytes 786432 | tf_op jit(solution)/shard_map/all_to_all | solution.py:44
  60.8 0.2 copy.55
  61.1 12.4 %all-to-all-done.1 = bf16[8,96,256]{2,0,1:T(8,128)(2,1)S(1)} async-done(((bf16[8,96,256]{2,0,1:T(8,128)(2,1)}), bf16[8,96,256]{2,0,1:T(8,128)(2,1)S(1)}, u32[]{:S(2)}, u32[]{:S(2)}) %all-to-all-start.1) | async-done | bytes 393248 | tf_op jit(solution)/shard_map/all_to_all | solution.py:44
  73.5 0.1 copy.53
  73.6 0.4 reshape.134
  74.0 0.4 fusion.12
  74.4 0.3 convolution_convert_fusion
  74.7 0.4 copy.57
  75.1 18.8 %all_to_all.60 = bf16[128,6,256]{2,1,0:T(8,128)(2,1)S(1)} all-to-all(bf16[128,6,256]{2,1,0:T(8,128)(2,1)S(1)} %copy.57), channel_id=1, replica_groups=mesh['member'=2,'lat'=4,'lon'=4] {'lat','lon'}, dimensions={0} | all-to-all | bytes 786432 | tf_op jit(solution)/shard_map/all_to_all | solution.py:70
  94.0 0.7 convert_bitcast_fusion
  94.8 2.5 %copy.61 = bf16[8,512,256]{2,0,1:T(8,128)(2,1)} copy(bf16[8,512,256]{2,1,0:T(8,128)(2,1)S(1)} %convert_bitcast_fusion) | data formatting | bytes 4194304 | tf_op jit(solution)/shard_map/convert_element_type | solution.py:73
  97.3 3.6 %all-to-all-start.3 = ((bf16[8,512,256]{2,0,1:T(8,128)(2,1)}), bf16[8,512,256]{2,0,1:T(8,128)(2,1)S(1)}, u32[]{:S(2)}, u32[]{:S(2)}) async-start(bf16[8,512,256]{2,0,1:T(8,128)(2,1)} %copy.61), calls=%async_computation.3 | async-start | bytes 4194304 | tf_op jit(solution)/shard_map/all_to_all | solution.py:75
  100.9 0.8 copy.56
  101.7 47.6 %all-to-all-done.3 = bf16[8,512,256]{2,0,1:T(8,128)(2,1)S(1)} async-done(((bf16[8,512,256]{2,0,1:T(8,128)(2,1)}), bf16[8,512,256]{2,0,1:T(8,128)(2,1)S(1)}, u32[]{:S(2)}, u32[]{:S(2)}) %all-to-all-start.3) | async-done | bytes 2097184 | tf_op jit(solution)/shard_map/all_to_all | solution.py:75
  149.3 0.6 copy.62
  149.9 1.0 copy-done.1
  150.9 11.1 %fusion.3 = bf16[32,128,256]{2,1,0:T(8,128)(2,1)} fusion(bf16[32,128,256]{2,1,0:T(8,128)(2,1)S(1)} %copy-done.1, f32[8,4,128,256]{3,2,0,1:T(8,128)S(1)} %copy.62, bf16[1,256,256]{2,1,0:T(8,128)(2,1)S(1)} %copy-done), kind=kOutput, calls=%fused_computation.4 | convolution fusion | flops 608174080 | bytes 8519680 | tf_op jit(solution)/shard_map/dot_general | solution.py:20
  (20 shorter events, 0.3 us)
Async XLA Ops:
  0.6 149.2 %copy-start = (bf16[1,256,256]{2,1,0:T(8,128)(2,1)S(1)}, bf16[1,256,256]{2,1,0:T(8,128)(2,1)}, u32[]{:S(2)}) copy-start(bf16[1,256,256]{2,1,0:T(8,128)(2,1)} %param.13) | copy-start | bytes 393220
  0.6 6.5 %copy-start.6 = (s32[48]{0:T(128)S(1)}, s32[48]{0:T(128)}, u32[]{:S(2)}) copy-start(s32[48]{0:T(128)} %param.8) | copy-start | bytes 580
  0.7 54.7 %all-to-all-start = ((bf16[32,128,256]{2,1,0:T(8,128)(2,1)}), bf16[32,128,256]{2,1,0:T(8,128)(2,1)S(1)}, u32[]{:S(2)}, u32[]{:S(2)}) async-start(bf16[32,128,256]{2,1,0:T(8,128)(2,1)} %param.7), calls=%async_computation | async-start | bytes 4194304 | tf_op jit(solution)/shard_map/all_to_all | solution.py:40
  7.8 52.9 %copy-start.2 = (bf16[1,2,256,256]{3,2,1,0:T(8,128)(2,1)S(1)}, bf16[1,2,256,256]{3,2,1,0:T(8,128)(2,1)}, u32[]{:S(2)}) copy-start(bf16[1,2,256,256]{3,2,1,0:T(8,128)(2,1)} %param.11) | copy-start | bytes 786436
  55.5 18.5 %copy-start.3 = (f32[1,48,256]{2,1,0:T(8,128)S(1)}, f32[1,48,256]{2,1,0:T(8,128)}, u32[]{:S(2)}) copy-start(f32[1,48,256]{2,1,0:T(8,128)} %param.12) | copy-start | bytes 147460
  55.5 18.5 %copy-start.4 = (bf16[3,48,128]{2,1,0:T(8,128)(2,1)S(1)}, bf16[3,48,128]{2,1,0:T(8,128)(2,1)}, u32[]{:S(2)}) copy-start(bf16[3,48,128]{2,1,0:T(8,128)(2,1)} %param.9) | copy-start | bytes 110596
  56.0 18.4 %copy-start.5 = (bf16[3,48,128]{2,1,0:T(8,128)(2,1)S(1)}, bf16[3,48,128]{2,1,0:T(8,128)(2,1)}, u32[]{:S(2)}) copy-start(bf16[3,48,128]{2,1,0:T(8,128)(2,1)} %param.10) | copy-start | bytes 110596
  57.0 16.5 %all-to-all-start.1 = ((bf16[8,96,256]{2,0,1:T(8,128)(2,1)}), bf16[8,96,256]{2,0,1:T(8,128)(2,1)S(1)}, u32[]{:S(2)}, u32[]{:S(2)}) async-start(bf16[8,96,256]{2,0,1:T(8,128)(2,1)} %copy.52), calls=%async_computation.1 | async-start | bytes 786432 | tf_op jit(solution)/shard_map/all_to_all | solution.py:44
  97.3 52.0 %all-to-all-start.3 = ((bf16[8,512,256]{2,0,1:T(8,128)(2,1)}), bf16[8,512,256]{2,0,1:T(8,128)(2,1)S(1)}, u32[]{:S(2)}, u32[]{:S(2)}) async-start(bf16[8,512,256]{2,0,1:T(8,128)(2,1)} %copy.61), calls=%async_computation.3 | async-start | bytes 4194304 | tf_op jit(solution)/shard_map/all_to_all | solution.py:75
  149.3 1.6 copy-start.1
where the time goes:
time: 162 us
  waiting for transfers between devices  108 us (67%)
  blocking collectives  18.8 us (12%)
  starting transfers between devices  13.9 us (9%)
  matrix products  13 us (8%)
  local copies, waits for them, and re-layouts  7.33 us (5%)
    all_to_all x1, waiting for transfers between devices, per_device(): lax.all_to_all(spectral, 'lon', split_axis=1, concat_axis=0, tiled=True)  47.6 us
    all_to_all x1, waiting for transfers between devices, per_device(): lax.all_to_all(current, 'lon', split_axis=0, concat_axis=1, tiled=True)  47.5 us
    all_to_all x1, blocking collectives, per_device(): lax.all_to_all(synthesized, ('lat', 'lon'), split_axis=0, concat_axis=1,...  18.8 us
    all_to_all x1, waiting for transfers between devices, per_device(): lax.all_to_all(lat_side, ('lat', 'lon'), split_axis=1, concat_axis=0, til...  12.4 us
    dot_general x1, matrix products, update(): jnp.dot(current.reshape(-1, shape_lead[-1]), skip_matrix, preferred_eleme...  11.1 us
    all_to_all x1, starting transfers between devices, per_device(): lax.all_to_all(current, 'lon', split_axis=0, concat_axis=1, tiled=True)  6.49 us
    all_to_all x1, starting transfers between devices, per_device(): lax.all_to_all(lat_side, ('lat', 'lon'), split_axis=1, concat_axis=0, til...  3.77 us
    all_to_all x1, starting transfers between devices, per_device(): lax.all_to_all(spectral, 'lon', split_axis=1, concat_axis=0, tiled=True)  3.61 us
  transfers between devices with their start and end apart: 3, of which 3 were waited for; matrix products, arithmetic and copies ran while one was open for 1% of the time, Pallas kernels for 0%

commit v1 on v0

--- a/solution.py
+++ b/solution.py
@@ -3,6 +3,18 @@
 import jax.numpy as jnp
 from jax import lax
 from jax.sharding import PartitionSpec as P
+
+
+def in_blocks(value, dim, size):
+    lengths = value.shape
+    pieces = value.reshape(*lengths[:dim], size, lengths[dim] // size, *lengths[dim + 1 :])
+    return jnp.moveaxis(pieces, dim, 0)
+
+
+def laid_out(tiles, dim):
+    shape = list(tiles.shape[1:])
+    shape[dim] *= tiles.shape[0]
+    return jnp.moveaxis(tiles, 0, dim).reshape(shape)
 
 
 def fourier_table(orders, length):
@@ -72,7 +84,15 @@
         "rqc,qk->rkc", returned, forward, preferred_element_type=jnp.float32
     ).astype(jnp.bfloat16)
     spectral, mixed_last = (spectral, mixed_modes)
-    grid_part = lax.all_to_all(spectral, "lon", split_axis=1, concat_axis=0, tiled=True)
+    size, index = (lax.axis_size("lon"), lax.axis_index("lon"))
+    blocks = in_blocks(spectral, 1, size)
+    out = blocks
+    for step in range(1, size):
+        target, source = ((index + step) % size, (index - step) % size)
+        sent = lax.dynamic_index_in_dim(blocks, target, 0)
+        received = lax.ppermute(sent, "lon", [(i, (i + step) % size) for i in range(size)])
+        out = lax.dynamic_update_slice_in_dim(out, received, source, axis=0)
+    grid_part = laid_out(out, 0)
     current = update(current, grid_part, skip_weight[0])
     return (current, mixed_last)
 

time: 162 us -> 156 us (0.963)
  the two profiles are of different devices: /device:TPU:0 before, /device:TPU:8 now
where the time goes in v1:
time: 156 us; the launch traced here: 155 us
  waiting for transfers between devices  110 us (71%)
  starting transfers between devices  22.3 us (14%)
  matrix products  13 us (8%)
  local copies, waits for them, and re-layouts  8.7 us (6%)
    all_to_all x1, waiting for transfers between devices, per_device(): lax.all_to_all(current, 'lon', split_axis=0, concat_axis=1, tiled=True)  44.3 us
    ppermute x3, waiting for transfers between devices, per_device(): lax.ppermute(sent, 'lon', [(i, (i + step) % size) for i in range(size)])  41.6 us
    all_to_all x1, waiting for transfers between devices, per_device(): lax.all_to_all(synthesized, ('lat', 'lon'), split_axis=0, concat_axis=1,...  13.5 us
    dot_general x1, matrix products, update(): jnp.dot(current.reshape(-1, shape_lead[-1]), skip_matrix, preferred_eleme...  11.1 us
    all_to_all x1, waiting for transfers between devices, per_device(): lax.all_to_all(lat_side, ('lat', 'lon'), split_axis=1, concat_axis=0, til...  10.6 us
    all_to_all x1, starting transfers between devices, per_device(): lax.all_to_all(lat_side, ('lat', 'lon'), split_axis=1, concat_axis=0, til...  6.95 us
    all_to_all x1, starting transfers between devices, per_device(): lax.all_to_all(current, 'lon', split_axis=0, concat_axis=1, tiled=True)  5.46 us
    all_to_all x1, starting transfers between devices, per_device(): lax.all_to_all(synthesized, ('lat', 'lon'), split_axis=0, concat_axis=1,...  5.26 us
  transfers between devices with their start and end apart: 6, of which 6 were waited for; matrix products, arithmetic and copies ran while one was open for 2% of the time, Pallas kernels for 0%

profile of v1, /device:TPU:8, one launch (start us, length us, event | category | flops | bytes accessed | tf_op | source)
XLA Modules:
  0.0 155.4 jit_solution(1275662339331810975)
XLA Ops:
  0.7 5.5 %all-to-all-start = ((bf16[32,128,256]{2,1,0:T(8,128)(2,1)}), bf16[32,128,256]{2,1,0:T(8,128)(2,1)S(1)}, u32[]{:S(2)}, u32[]{:S(2)}) async-start(bf16[32,128,256]{2,1,0:T(8,128)(2,1)} %param.7), calls=%async_computation | async-start | bytes 4194304 | tf_op jit(solution)/shard_map/all_to_all | solution.py:52
  6.1 0.5 cosine_convert_fusion
  6.8 44.3 %all-to-all-done = bf16[32,128,256]{2,1,0:T(8,128)(2,1)S(1)} async-done(((bf16[32,128,256]{2,1,0:T(8,128)(2,1)}), bf16[32,128,256]{2,1,0:T(8,128)(2,1)S(1)}, u32[]{:S(2)}, u32[]{:S(2)}) %all-to-all-start) | async-done | bytes 2097184 | tf_op jit(solution)/shard_map/all_to_all | solution.py:52
  51.2 0.5 fusion.11
  51.7 1.0 copy.50
  52.7 7.0 %all-to-all-start.1 = ((bf16[8,96,256]{2,0,1:T(8,128)(2,1)}), bf16[8,96,256]{2,0,1:T(8,128)(2,1)S(1)}, u32[]{:S(2)}, u32[]{:S(2)}) async-start(bf16[8,96,256]{2,0,1:T(8,128)(2,1)} %copy.50), calls=%async_computation.1 | async-start | bytes 786432 | tf_op jit(solution)/shard_map/all_to_all | solution.py:56
  59.9 10.6 %all-to-all-done.1 = bf16[8,96,256]{2,0,1:T(8,128)(2,1)S(1)} async-done(((bf16[8,96,256]{2,0,1:T(8,128)(2,1)}), bf16[8,96,256]{2,0,1:T(8,128)(2,1)S(1)}, u32[]{:S(2)}, u32[]{:S(2)}) %all-to-all-start.1) | async-done | bytes 393248 | tf_op jit(solution)/shard_map/all_to_all | solution.py:56
  71.1 0.4 fusion.12
  71.8 1.2 copy.55
  73.0 5.3 %all-to-all-start.2 = ((bf16[128,6,256]{2,1,0:T(8,128)(2,1)}), bf16[128,6,256]{2,1,0:T(8,128)(2,1)S(1)}, u32[]{:S(2)}, u32[]{:S(2)}) async-start(bf16[128,6,256]{2,1,0:T(8,128)(2,1)} %copy.55), calls=%async_computation.2 | async-start | bytes 1048576 | tf_op jit(solution)/shard_map/all_to_all | solution.py:82
  78.3 13.5 %all-to-all-done.2 = bf16[128,6,256]{2,1,0:T(8,128)(2,1)S(1)} async-done(((bf16[128,6,256]{2,1,0:T(8,128)(2,1)}), bf16[128,6,256]{2,1,0:T(8,128)(2,1)S(1)}, u32[]{:S(2)}, u32[]{:S(2)}) %all-to-all-start.2) | async-done | bytes 393248 | tf_op jit(solution)/shard_map/all_to_all | solution.py:82
  91.9 0.7 convolution_convert_fusion
  92.6 0.9 dynamic-slice_bitcast_fusion
  93.5 0.5 collective-permute-start
  94.1 4.0 %collective-permute-start.1 = (bf16[1,8,128,256]{3,2,0,1:T(8,128)(2,1)S(1)}, bf16[1,8,128,256]{3,2,0,1:T(8,128)(2,1)}, u32[]{:S(2)}, u32[]{:S(2)}) collective-permute-start(bf16[1,8,128,256]{3,2,0,1:T(8,128)(2,1)S(1)} %get-tuple-element.13), channel_id=1, source_target_pairs={{0,2},{1,3},{2,0},{3,1},{4,6},{5,7},{6,4},{7,5},{8,10},{9,11},{10,... | collective-permute-start | bytes 1572872 | tf_op jit(solution)/shard_map/ppermute | solution.py:93
  98.1 0.8 copy.54
  98.9 9.9 %collective-permute-done = bf16[1,8,128,256]{3,2,0,1:T(8,128)(2,1)} collective-permute-done((bf16[1,8,128,256]{3,2,0,1:T(8,128)(2,1)}, bf16[1,8,128,256]{3,2,0,1:T(8,128)(2,1)}, u32[]{:S(2)}, u32[]{:S(2)}) %collective-permute-start) | collective-permute-done | bytes 524320 | tf_op jit(solution)/shard_map/ppermute | solution.py:93
  108.9 1.1 constant_dynamic-update-slice_fusion.2
  109.9 29.9 %collective-permute-done.1 = bf16[1,8,128,256]{3,2,0,1:T(8,128)(2,1)} collective-permute-done((bf16[1,8,128,256]{3,2,0,1:T(8,128)(2,1)S(1)}, bf16[1,8,128,256]{3,2,0,1:T(8,128)(2,1)}, u32[]{:S(2)}, u32[]{:S(2)}) %collective-permute-start.1) | collective-permute-done | bytes 524320 | tf_op jit(solution)/shard_map/ppermute | solution.py:93
  139.9 1.1 constant_dynamic-update-slice_fusion.1
  141.0 1.7 %collective-permute-done.2 = bf16[1,8,128,256]{3,2,0,1:T(8,128)(2,1)} collective-permute-done((bf16[1,8,128,256]{3,2,0,1:T(8,128)(2,1)S(1)}, bf16[1,8,128,256]{3,2,0,1:T(8,128)(2,1)}, u32[]{:S(2)}, u32[]{:S(2)}) %collective-permute-start.2) | collective-permute-done | bytes 524320 | tf_op jit(solution)/shard_map/ppermute | solution.py:93
  142.7 1.1 constant_dynamic-update-slice_fusion
  143.8 0.5 copy.59
  144.3 11.1 %fusion.3 = bf16[32,128,256]{2,1,0:T(8,128)(2,1)} fusion(bf16[32,128,256]{2,1,0:T(8,128)(2,1)S(1)} %copy-done.1, f32[4,8,128,256]{3,2,1,0:T(8,128)S(1)} %copy.59, bf16[1,256,256]{2,1,0:T(8,128)(2,1)S(1)} %copy-done), kind=kOutput, calls=%fused_computation.4 | convolution fusion | flops 608174080 | bytes 8519680 | tf_op jit(solution)/shard_map/dot_general | solution.py:32
  (28 shorter events, 1.5 us)
Async XLA Ops:
  0.6 143.6 %copy-start = (bf16[1,256,256]{2,1,0:T(8,128)(2,1)S(1)}, bf16[1,256,256]{2,1,0:T(8,128)(2,1)}, u32[]{:S(2)}) copy-start(bf16[1,256,256]{2,1,0:T(8,128)(2,1)} %param.13) | copy-start | bytes 393220
  0.6 5.5 %copy-start.6 = (s32[48]{0:T(128)S(1)}, s32[48]{0:T(128)}, u32[]{:S(2)}) copy-start(s32[48]{0:T(128)} %param.8) | copy-start | bytes 580
  0.7 50.4 %all-to-all-start = ((bf16[32,128,256]{2,1,0:T(8,128)(2,1)}), bf16[32,128,256]{2,1,0:T(8,128)(2,1)S(1)}, u32[]{:S(2)}, u32[]{:S(2)}) async-start(bf16[32,128,256]{2,1,0:T(8,128)(2,1)} %param.7), calls=%async_computation | async-start | bytes 4194304 | tf_op jit(solution)/shard_map/all_to_all | solution.py:52
  6.8 52.8 %copy-start.2 = (bf16[1,2,256,256]{3,2,1,0:T(8,128)(2,1)S(1)}, bf16[1,2,256,256]{3,2,1,0:T(8,128)(2,1)}, u32[]{:S(2)}) copy-start(bf16[1,2,256,256]{3,2,1,0:T(8,128)(2,1)} %param.11) | copy-start | bytes 786436
  51.2 19.9 %copy-start.3 = (f32[1,48,256]{2,1,0:T(8,128)S(1)}, f32[1,48,256]{2,1,0:T(8,128)}, u32[]{:S(2)}) copy-start(f32[1,48,256]{2,1,0:T(8,128)} %param.12) | copy-start | bytes 147460
  51.2 19.9 %copy-start.4 = (bf16[3,48,128]{2,1,0:T(8,128)(2,1)S(1)}, bf16[3,48,128]{2,1,0:T(8,128)(2,1)}, u32[]{:S(2)}) copy-start(bf16[3,48,128]{2,1,0:T(8,128)(2,1)} %param.9) | copy-start | bytes 110596
  51.7 19.8 %copy-start.5 = (bf16[3,48,128]{2,1,0:T(8,128)(2,1)S(1)}, bf16[3,48,128]{2,1,0:T(8,128)(2,1)}, u32[]{:S(2)}) copy-start(bf16[3,48,128]{2,1,0:T(8,128)(2,1)} %param.10) | copy-start | bytes 110596
  52.7 17.9 %all-to-all-start.1 = ((bf16[8,96,256]{2,0,1:T(8,128)(2,1)}), bf16[8,96,256]{2,0,1:T(8,128)(2,1)S(1)}, u32[]{:S(2)}, u32[]{:S(2)}) async-start(bf16[8,96,256]{2,0,1:T(8,128)(2,1)} %copy.50), calls=%async_computation.1 | async-start | bytes 786432 | tf_op jit(solution)/shard_map/all_to_all | solution.py:56
  73.0 18.8 %all-to-all-start.2 = ((bf16[128,6,256]{2,1,0:T(8,128)(2,1)}), bf16[128,6,256]{2,1,0:T(8,128)(2,1)S(1)}, u32[]{:S(2)}, u32[]{:S(2)}) async-start(bf16[128,6,256]{2,1,0:T(8,128)(2,1)} %copy.55), calls=%async_computation.2 | async-start | bytes 1048576 | tf_op jit(solution)/shard_map/all_to_all | solution.py:82
  93.5 15.3 %collective-permute-start = (bf16[1,8,128,256]{3,2,0,1:T(8,128)(2,1)}, bf16[1,8,128,256]{3,2,0,1:T(8,128)(2,1)}, u32[]{:S(2)}, u32[]{:S(2)}) collective-permute-start(bf16[1,8,128,256]{3,2,0,1:T(8,128)(2,1)} %get-tuple-element.14), channel_id=1, source_target_pairs={{0,1},{1,2},{2,3},{3,0},{4,5},{5,6},{6,7},{7,4},{8,9},{9,10},{10,1... | collective-permute-start | bytes 1572872 | tf_op jit(solution)/shard_map/ppermute | solution.py:93
  94.1 45.8 %collective-permute-start.1 = (bf16[1,8,128,256]{3,2,0,1:T(8,128)(2,1)S(1)}, bf16[1,8,128,256]{3,2,0,1:T(8,128)(2,1)}, u32[]{:S(2)}, u32[]{:S(2)}) collective-permute-start(bf16[1,8,128,256]{3,2,0,1:T(8,128)(2,1)S(1)} %get-tuple-element.13), channel_id=1, source_target_pairs={{0,2},{1,3},{2,0},{3,1},{4,6},{5,7},{6,4},{7,5},{8,10},{9,11},{10,... | collective-permute-start | bytes 1572872 | tf_op jit(solution)/shard_map/ppermute | solution.py:93
  98.1 44.6 %collective-permute-start.2 = (bf16[1,8,128,256]{3,2,0,1:T(8,128)(2,1)S(1)}, bf16[1,8,128,256]{3,2,0,1:T(8,128)(2,1)}, u32[]{:S(2)}, u32[]{:S(2)}) collective-permute-start(bf16[1,8,128,256]{3,2,0,1:T(8,128)(2,1)S(1)} %get-tuple-element.12), channel_id=1, source_target_pairs={{0,3},{1,0},{2,1},{3,2},{4,7},{5,4},{6,5},{7,6},{8,11},{9,8},{10,9... | collective-permute-start | bytes 1572872 | tf_op jit(solution)/shard_map/ppermute | solution.py:93
  109.9 34.4 %copy-start.1 = (bf16[32,128,256]{2,1,0:T(8,128)(2,1)S(1)}, bf16[32,128,256]{2,1,0:T(8,128)(2,1)}, u32[]{:S(2)}) copy-start(bf16[32,128,256]{2,1,0:T(8,128)(2,1)} %param.7) | copy-start | bytes 6291460
